TPU v7x, 32 devices: a whole 2x2x4 slice. The times are simulated.
32 devices in a mesh: row: 4 (over y, x), col: 8 (over z, core).
Axes of the slice: x: 2, y: 2, z: 4, core: 2. Of those that a mesh axis runs over, the one named last changes fastest.
Arguments:
- features: bfloat16 [32768, 128], P(('row', 'col')), may hold values from -24 to 24
- tile_rows: int32 [4, 8, 1024], P('row', 'col'), may hold values from 0 to 63
- tile_cols: int32 [4, 8, 1024], P('row', 'col'), may hold values from 0 to 31
- edge_lists: int32 [2, 4, 8, 1024, 128], P(None, 'row', 'col'), may hold values from -16 to 127
- tile_counts: int32 [4, 8], P('row', 'col'), may hold values from 128 to 1024, as said below
Outputs:
- hop_one: bfloat16 [32768, 128], P(('row', 'col'))
- hop_two: bfloat16 [32768, 128], P(('row', 'col'))
Inputs may be any that keep to these rules, and one draw needn't show every extreme that they name: `tile_counts`: live tile slots of a block; some block has exactly 1024. `edge_lists`: a negative entry marks an empty edge slot; slots at or past a block's count hold arbitrary entries. `tile_rows`: a tile may occur in several slots; slots at or past a block's count hold arbitrary entries. `tile_cols`: slots at or past a block's count hold arbitrary entries.
All inputs are finite; a program needn't handle non-finite values.
Results may differ from a plain program's by a relative error of at most 0.0058.
Values may be sent and summed in bfloat16 or wider, within the bound.
A program may use at most 192 MiB of HBM per device.

v0:
```python
import functools

import jax
import jax.numpy as jnp
from jax import lax
from jax.experimental import pallas as pl
from jax.experimental.pallas import tpu as pltpu
from jax.sharding import PartitionSpec as P

TILE = 128
ROWS_MIN = 16
BUILD_UNROLL = 32
APPLY_UNROLL = 32
APPLY_SLOTS = 4
HOT = jnp.float8_e4m3fn
HOT_EXTRA = 32
EXTRA = 16
PIECES = 4
CORES = 2
MESH_ID = pl.DeviceIdType.MESH
VMEM_SPEC = pl.BlockSpec(memory_space=pltpu.VMEM)
SMEM_SPEC = pl.BlockSpec(memory_space=pltpu.SMEM)
ANY_SPEC = pl.BlockSpec(memory_space=pl.ANY)


def place_of():
    row, col = lax.axis_index("row"), lax.axis_index("col")
    return row, col, lax.rem(col, CORES), col // CORES


def order_kernel(own, n_chip, count_ref, rows_ref, cols_ref, order_ref):
    slots = rows_ref.shape[-1]
    places = order_ref.shape[-1]
    bins = CORES * n_chip * own
    bf16, f32 = jnp.bfloat16, jnp.float32
    _, _, core, chip = place_of()

    def iota(shape, dim):
        return lax.broadcasted_iota(jnp.int32, shape, dim)

    def hot(mask):
        return jnp.where(mask, 1.0, 0.0).astype(bf16)

    def mul(x, y):
        return jnp.dot(x.astype(bf16), y.astype(bf16), preferred_element_type=f32)

    slot = iota((1, slots), 1)
    alive = slot < count_ref[0]
    rows = jnp.where(alive, rows_ref[...], 0)
    cols = jnp.where(alive, cols_ref[...], 0)
    owner = rows // own
    target = owner // CORES
    other = jnp.where(lax.rem(owner, CORES) == core, 0, 1)
    rank = jnp.where(chip < n_chip // 2, n_chip - 1 - target, target)
    within = lax.rem(rows, own)
    bin_of = jnp.where(alive, (other * n_chip + rank) * own + within, -1)
    local = target * own + within
    belongs = bin_of == iota((bins, slots), 0)
    ranks = mul(hot(belongs), hot(iota((slots, slots), 0) <= iota((slots, slots), 1)))
    totals = jnp.broadcast_to(ranks[:, slots - 1 :], (bins, TILE)).astype(jnp.int32)
    pairs = (totals + 1) // 2
    before = hot(iota((bins, bins), 1) < iota((bins, bins), 0))
    offsets = 2.0 * (
        32.0 * mul(before, (pairs // 32).astype(f32)) + mul(before, (pairs % 32).astype(f32))
    )
    spots = jnp.where(belongs, ranks - 1.0 + offsets[:, :1], 0.0)
    spot = jnp.where(alive, jnp.sum(spots, axis=0, keepdims=True), -1.0)
    spot = jnp.broadcast_to(spot, (TILE, slots)).T.astype(jnp.int32)
    facts = [slot // 32, slot % 32, jnp.where(alive, 1, 0), local, cols]
    facts = jnp.concatenate(
        [fact.astype(f32) for fact in facts] + [jnp.zeros((EXTRA - len(facts), slots), f32)], axis=0
    )
    for block in range(places // TILE):
        taken = hot(spot == iota((slots, TILE), 1) + block * TILE)
        found = mul(facts, taken).astype(jnp.int32)
        place = 32 * found[0:1] + found[1:2] + found[2:3] - 1
        order_ref[:, block * TILE : (block + 1) * TILE] = jnp.concatenate(
            [place, found[3:5], jnp.zeros((5, TILE), jnp.int32)], axis=0
        )
    order_ref[3:4, 0:bins] = offsets.T[0:1, :].astype(jnp.int32)
    end = jnp.sum(2.0 * pairs.astype(f32), axis=0, keepdims=True).astype(jnp.int32)
    order_ref[4:5, 0:TILE] = end


def span_of(order_ref, half_bins, other):
    middle = order_ref[3, half_bins]
    if other:
        return middle, order_ref[4, 0]
    return 0, middle


def build_kernel(half_bins, other, order_ref, dst_ref, src_ref, store_ref, degree_ref, made, degree_acc, sem):
    degree_acc[...] = jnp.zeros_like(degree_acc)
    low, high = span_of(order_ref, half_bins, other)
    turns = (high - low + BUILD_UNROLL - 1) // BUILD_UNROLL
    pairs = BUILD_UNROLL // 2
    cells = lax.broadcasted_iota(jnp.int32, (TILE, TILE), 0)

    def out_copy(turn):
        side = lax.rem(turn, 2)
        return pltpu.make_async_copy(
            made.at[side], store_ref.at[pl.ds(turn * pairs, pairs)], sem.at[side]
        )

    def visit(turn, carry):
        side = lax.rem(turn, 2)

        @pl.when(turn >= 2)
        def _():
            out_copy(turn - 2).wait()

        for pair in range(pairs):
            counts = []
            base = low + turn * BUILD_UNROLL + 2 * pair
            for half in range(2):
                slot = jnp.where(base < high, order_ref[0, base + half], -1)
                safe = jnp.maximum(slot, 0)
                dst = jnp.where(slot >= 0, dst_ref[pl.ds(safe, 1), :], -1)
                src = src_ref[pl.ds(safe, 1), :]
                dst_hot = jnp.where(dst == cells, 1.0, 0.0).astype(HOT)
                src_hot = jnp.where(src == cells, 1.0, 0.0).astype(HOT)
                valid = jnp.broadcast_to(jnp.where(src >= 0, 1.0, 0.0), (HOT_EXTRA, TILE))
                left = jnp.concatenate([src_hot, valid.astype(HOT)], axis=0)
                both = lax.dot_general(
                    left, dst_hot, (((1,), (1,)), ((), ())), preferred_element_type=jnp.float32
                )
                made[side, pair, half * TILE : (half + 1) * TILE] = both[:TILE].astype(jnp.bfloat16)
                counts.append(both[TILE : TILE + 8])
            degree_acc[order_ref[1, base]] += counts[0] + counts[1]
        out_copy(turn).start()
        return carry

    lax.fori_loop(0, turns, visit, 0)

    @pl.when(turns >= 2)
    def _():
        out_copy(turns - 2).wait()

    @pl.when(turns >= 1)
    def _():
        out_copy(turns - 1).wait()

    degree_ref[...] = degree_acc[:, 0, :]


def apply_kernel(half_bins, orders, stores, source_ref, out_ref, held, acc, sem):
    acc[...] = jnp.zeros_like(acc)
    pairs = APPLY_UNROLL // 2
    spans = [span_of(order, half_bins, other) for other, order in enumerate(orders)]
    turns = [(high - low + APPLY_UNROLL - 1) // APPLY_UNROLL for low, high in spans]
    total = turns[0] + turns[1]

    def fetch(turn):
        slot = lax.rem(turn, APPLY_SLOTS)
        for other in range(2):
            local = turn - other * turns[0]

            @pl.when((local >= 0) & (local < turns[other]))
            def _():
                pltpu.make_async_copy(
                    stores[other].at[pl.ds(local * pairs, pairs)], held.at[slot], sem.at[slot]
                ).start()

    for turn in range(APPLY_SLOTS - 1):
        fetch(turn)

    for other in range(2):
        order_ref = orders[other]
        low, high = spans[other]
        offset = other * source_ref.shape[0] // 2

        def visit(turn, carry):
            slot = lax.rem(turn, APPLY_SLOTS)
            pltpu.make_async_copy(
                stores[0].at[pl.ds(0, pairs)], held.at[slot], sem.at[slot]
            ).wait()
            fetch(turn + APPLY_SLOTS - 1)
            for pair in range(pairs):
                base = low + (turn - other * turns[0]) * APPLY_UNROLL + 2 * pair
                sources = jnp.concatenate(
                    [
                        source_ref[offset + order_ref[2, base]],
                        source_ref[offset + order_ref[2, base + 1]],
                    ],
                    axis=1,
                )
                acc[order_ref[1, base]] += jnp.dot(
                    sources, held[slot, pair], preferred_element_type=jnp.float32
                )
            return carry

        lax.fori_loop(other * turns[0], turns[0] + other * turns[1], visit, 0)
    out_ref[...] = acc[...].astype(jnp.bfloat16)


def greet(targets):
    barrier = pltpu.get_barrier_semaphore()
    for target in targets:
        pl.semaphore_signal(barrier, inc=1, device_id=target, device_id_type=MESH_ID)
    pl.semaphore_wait(barrier, len(targets))


def row_peers(n_row, side=0):
    row, col, core, chip = place_of()
    if side:
        col = chip * CORES + 1 - core
    return [(lax.rem(row + d, n_row), col) for d in range(1, n_row)]


def sibling_peers(n_col):
    row, col, _, _ = place_of()
    return [(row, lax.rem(col + CORES * d, n_col)) for d in range(1, n_col // CORES)]


def partner_of():
    row, col, core, chip = place_of()
    return (row, chip * CORES + 1 - core)


def remote(src, dst, send_sem, recv_sem, target):
    return pltpu.make_async_remote_copy(
        src_ref=src,
        dst_ref=dst,
        send_sem=send_sem,
        recv_sem=recv_sem,
        device_id=target,
        device_id_type=MESH_ID,
    )


def send(*args):
    copy = remote(*args)
    copy.start()
    return copy


def prep_kernel(features_ref, out_ref):
    for tile in range(out_ref.shape[0]):
        block = features_ref[tile * TILE : (tile + 1) * TILE, :].astype(jnp.float32).T
        out_ref[tile] = block.astype(jnp.bfloat16)


def start_kernel(n_row, n_col, deg_a_ref, deg_b_ref, *refs):
    blocks = refs[:n_row]
    gathered_ref, root_ref, part, taken, theirs, roots = refs[n_row : n_row + 6]
    deg_send, deg_recv, near_send, near_recv, root_send, root_recv = refs[n_row + 6 :]
    row, col, core, chip = place_of()
    n_chip = n_col // CORES
    own = root_ref.shape[0]
    partner = partner_of()
    siblings = sibling_peers(n_col)
    mine, cross = row_peers(n_row), row_peers(n_row, 1)
    greet(siblings + mine + cross + [partner])
    part[...] = deg_a_ref[...] + deg_b_ref[...]
    copies = []
    for d, target in enumerate(siblings):
        start = (target[1] // CORES) * own
        copies.append(
            send(
                part.at[pl.ds(pl.multiple_of(start, own), own)],
                taken.at[d],
                deg_send.at[d],
                deg_recv.at[d],
                target,
            )
        )
    near = []
    for d in range(n_row):
        near.append(send(blocks[d], theirs.at[d], near_send.at[d], near_recv.at[d], partner))
    degree = part[pl.ds(pl.multiple_of(chip * own, own), own), :]
    for d, copy in enumerate(copies):
        copy.wait_recv()
        degree = degree + taken[d]
    root = lax.rsqrt(1.0 + degree)
    root_ref[...] = root
    roots[0, 0] = root
    root_copies = []
    for side, targets in ((0, mine), (1, [partner] + cross)):
        for d, target in enumerate(targets):
            d += 1 - side
            root_copies.append(
                send(roots.at[0, 0], roots.at[side, d], root_send.at[side, d], root_recv.at[side, d], target)
            )

    def scale(side, d, source, root):
        start = side * n_row * own + lax.rem(row + n_row - d, n_row) * own
        for tile in range(own):
            gathered_ref[start + tile] = (
                source[tile].astype(jnp.float32) * root[tile : tile + 1, :]
            ).astype(jnp.bfloat16)

    scale(0, 0, blocks[0], root)
    for copy in root_copies:
        copy.wait_recv()
    for d in range(1, n_row):
        scale(0, d, blocks[d], roots[0, d])
    for d in range(n_row):
        near[d].wait_recv()
        scale(1, d, theirs.at[d], roots[1, d])
    for copy in copies + near + root_copies:
        copy.wait_send()


def sum_kernel(n_row, n_col, spread, part_ref, root_ref, *refs):
    if spread:
        hop_ref, gathered_ref, comes, goes, *sems = refs
        send_sem, recv_sem, row_send, row_recv, near_send, near_recv = sems
    else:
        hop_ref, comes, goes, send_sem, recv_sem = refs
    row, col, core, chip = place_of()
    n_chip = n_col // CORES
    own = root_ref.shape[0]
    size = own // PIECES
    partner = partner_of()
    up = (row, lax.rem(col + CORES, n_col))
    down = (row, lax.rem(col + n_col - CORES, n_col))
    mine = row_peers(n_row)
    greet([up, down] + ([partner] + mine if spread else []))
    last = n_chip - 1

    def hop_copy(way, k, piece, direct):
        target = last - k if way == 0 else k
        source = (
            part_ref.at[pl.ds(target * own + piece * size, size)] if direct else goes.at[way, k, piece]
        )
        return remote(
            source,
            comes.at[way, k, piece],
            send_sem.at[way, k, piece],
            recv_sem.at[way, k, piece],
            down if way else up,
        )

    def steps():
        for k in range(last):
            for piece in range(PIECES):
                for way in range(2):
                    target = last - k if way == 0 else k
                    ahead = (chip < target) if way == 0 else (chip > target)
                    first = chip == (0 if way == 0 else last)
                    yield k, piece, way, target, ahead, first

    for k, piece, way, target, ahead, first in steps():

        @pl.when(ahead & first)
        def _():
            hop_copy(way, k, piece, True).start()

        @pl.when(ahead & jnp.logical_not(first))
        def _():
            hop_copy(way, k, piece, False).wait_recv()
            start = target * own + piece * size
            goes[way, k, piece] = (
                part_ref[start : start + size].astype(jnp.float32)
                + comes[way, k, piece].astype(jnp.float32)
            ).astype(jnp.bfloat16)
            hop_copy(way, k, piece, False).start()

    row_copies, near_copies = {}, {}
    for piece in range(PIECES):
        for way, k, fed in ((0, last - chip, chip > 0), (1, chip, chip < last)):

            @pl.when(fed)
            def _():
                hop_copy(way, k, piece, False).wait_recv()

        total = part_ref[pl.ds(chip * own + piece * size, size)].astype(jnp.float32)
        below = comes[0, jnp.minimum(last - chip, last - 1), piece].astype(jnp.float32)
        above = comes[1, jnp.minimum(chip, last - 1), piece].astype(jnp.float32)
        total = total + jnp.where(chip > 0, below, 0.0) + jnp.where(chip < last, above, 0.0)
        roots = [root_ref[piece * size + tile : piece * size + tile + 1, :] for tile in range(size)]
        if spread:
            start = row * own + piece * size
            for tile in range(size):
                gathered_ref[start + tile] = (total[tile] * (roots[tile] * roots[tile])).astype(
                    jnp.bfloat16
                )
            for d, target in enumerate(mine):
                place = gathered_ref.at[pl.ds(start, size)]
                row_copies[piece, d] = send(
                    place, place, row_send.at[piece, d], row_recv.at[piece, d], target
                )
            near_copies[piece, 0] = send(
                gathered_ref.at[pl.ds(start, size)],
                gathered_ref.at[pl.ds(n_row * own + start, size)],
                near_send.at[piece, 0],
                near_recv.at[piece, 0],
                partner,
            )
        for tile in range(size):
            place = (piece * size + tile) * TILE
            hop_ref[place : place + TILE, :] = (total[tile] * roots[tile]).T.astype(jnp.bfloat16)
    for (piece, d), copy in row_copies.items():
        copy.wait_recv()
        start = lax.rem(row + n_row - d - 1, n_row) * own + piece * size
        near_copies[piece, d + 1] = send(
            gathered_ref.at[pl.ds(start, size)],
            gathered_ref.at[pl.ds(n_row * own + start, size)],
            near_send.at[piece, d + 1],
            near_recv.at[piece, d + 1],
            partner,
        )
    for copy in near_copies.values():
        copy.wait_recv()
    for copy in list(row_copies.values()) + list(near_copies.values()):
        copy.wait_send()
    for k, piece, way, target, ahead, first in steps():

        @pl.when(ahead)
        def _():
            hop_copy(way, k, piece, False).wait_send()


def sems(*shape):
    return pltpu.SemaphoreType.DMA(shape)


def comm_params(ident):
    return pltpu.CompilerParams(
        collective_id=ident, has_side_effects=True, vmem_limit_bytes=48 * 2**20
    )


def plain_params():
    return pltpu.CompilerParams(vmem_limit_bytes=48 * 2**20)


def local(features, tile_rows, tile_cols, edge_lists, tile_counts):
    node_count, feat_width = features.shape
    n_row, n_col = lax.axis_size("row"), lax.axis_size("col")
    n_chip = n_col // CORES
    own = node_count // TILE
    half_tiles = own * n_chip
    source_tiles = own * n_row
    slots = tile_rows.shape[-1]
    bf16, f32 = jnp.bfloat16, jnp.float32
    places = -(-(slots + CORES * half_tiles) // TILE) * TILE
    swap = [(i, i + 1 - 2 * (i % CORES)) for i in range(n_col)]

    edges_b = lax.ppermute(edge_lists, "col", swap)
    own_type = jax.ShapeDtypeStruct((own, feat_width, TILE), bf16)
    turned = pl.pallas_call(
        prep_kernel,
        out_shape=own_type,
        in_specs=[VMEM_SPEC],
        out_specs=VMEM_SPEC,
        name="prep",
    )(features)
    blocks = [turned] + [
        lax.ppermute(turned, "row", [(i, (i + d) % n_row) for i in range(n_row)])
        for d in range(1, n_row)
    ]

    order = pl.pallas_call(
        functools.partial(order_kernel, own, n_chip),
        out_shape=jax.ShapeDtypeStruct((8, places), jnp.int32),
        in_specs=[SMEM_SPEC, VMEM_SPEC, VMEM_SPEC],
        out_specs=VMEM_SPEC,
        compiler_params=plain_params(),
        name="order",
    )(tile_counts[0], tile_rows[0], tile_cols[0])
    order_b = lax.ppermute(order, "col", swap)

    def build(order, edges, other):
        edges = edges.reshape(2, slots, TILE)
        return pl.pallas_call(
            functools.partial(build_kernel, half_tiles, other),
            in_specs=[SMEM_SPEC]
            + [
                pl.BlockSpec((None, slots, TILE), lambda i, side=side: (side, 0, 0))
                for side in range(2)
            ],
            grid=(1,),
            out_specs=[ANY_SPEC, pl.BlockSpec((half_tiles, TILE), lambda i: (0, 0))],
            scratch_shapes=[
                pltpu.VMEM((2, BUILD_UNROLL // 2, 2 * TILE, TILE), bf16),
                pltpu.VMEM((half_tiles, 8, TILE), f32),
                sems(2),
            ],
            out_shape=[
                jax.ShapeDtypeStruct((places // 2, 2 * TILE, TILE), bf16),
                jax.ShapeDtypeStruct((half_tiles, TILE), f32),
            ],
            compiler_params=plain_params(),
            cost_estimate=pl.CostEstimate(flops=10**10, bytes_accessed=0, transcendentals=0),
            name="build",
        )(order, edges, edges)

    store_a, degree_a = build(order, edge_lists, False)
    store_b, degree_b = build(order_b, edges_b, True)

    gathered_type = jax.ShapeDtypeStruct((CORES * source_tiles, feat_width, TILE), bf16)
    gathered, root = pl.pallas_call(
        functools.partial(start_kernel, n_row, n_col),
        out_shape=[gathered_type, jax.ShapeDtypeStruct((own, TILE), f32)],
        in_specs=[VMEM_SPEC] * (2 + n_row),
        out_specs=[VMEM_SPEC] * 2,
        scratch_shapes=[
            pltpu.VMEM((half_tiles, TILE), f32),
            pltpu.VMEM((n_chip - 1, own, TILE), f32),
            pltpu.VMEM((n_row, own, feat_width, TILE), bf16),
            pltpu.VMEM((2, n_row, own, TILE), f32),
            sems(n_chip - 1),
            sems(n_chip - 1),
            sems(n_row),
            sems(n_row),
            sems(2, n_row),
            sems(2, n_row),
        ],
        compiler_params=comm_params(0),
        name="start",
    )(degree_a, degree_b, *blocks)

    def apply(sources):
        def body(order_a, order_b, store_a, store_b, *refs):
            apply_kernel(half_tiles, (order_a, order_b), (store_a, store_b), *refs)

        return pl.pallas_call(
            body,
            in_specs=[SMEM_SPEC] * 2 + [ANY_SPEC] * 2 + [VMEM_SPEC],
            out_specs=VMEM_SPEC,
            scratch_shapes=[
                pltpu.VMEM((APPLY_SLOTS, APPLY_UNROLL // 2, 2 * TILE, TILE), bf16),
                pltpu.VMEM((half_tiles, feat_width, TILE), f32),
                sems(APPLY_SLOTS),
            ],
            out_shape=jax.ShapeDtypeStruct((half_tiles, feat_width, TILE), bf16),
            compiler_params=plain_params(),
            name="apply",
        )(order, order_b, store_a, store_b, sources)

    def collect(part, spread):
        size = own // PIECES
        outs = [jax.ShapeDtypeStruct((node_count, feat_width), bf16)]
        semaphores = [sems(2, n_chip - 1, PIECES)] * 2
        if spread:
            outs.append(gathered_type)
            semaphores += [sems(PIECES, n_row - 1)] * 2 + [sems(PIECES, n_row)] * 2
        return pl.pallas_call(
            functools.partial(sum_kernel, n_row, n_col, spread),
            out_shape=outs,
            in_specs=[VMEM_SPEC] * 2,
            out_specs=[VMEM_SPEC] * len(outs),
            scratch_shapes=[pltpu.VMEM((2, n_chip - 1, PIECES, size, feat_width, TILE), bf16)] * 2
            + semaphores,
            compiler_params=comm_params(1 if spread else 2),
            name="spread" if spread else "finish",
        )(part, root)

    hop_one, gathered = collect(apply(gathered), True)
    (hop_two,) = collect(apply(gathered), False)
    return (hop_one, hop_two)


def solution(mesh):
    placed = (
        P(("row", "col"), None),
        P("row", "col", None),
        P("row", "col", None),
        P(None, "row", "col", None, None),
        P("row", "col"),
    )
    return jax.shard_map(
        local,
        mesh=mesh,
        in_specs=placed,
        out_specs=(P(("row", "col"), None), P(("row", "col"), None)),
        check_vma=False,
    )
```

profile of v0, /device:TPU:18, one launch (start us, length us, event | category | flops | bytes accessed | tf_op | source)
XLA Modules:
  0.0 148.8 jit_solution(6887765044085263596)
XLA Ops:
  0.6 0.1 collective-permute-start.1
  0.7 1.8 %prep.1.refs_0_ = bf16[8,128,128]{2,1,0:T(8,128)(2,1)} custom-call(bf16[1024,128]{1,0:T(8,128)(2,1)} %features_ref.1), custom_call_target="tpu_custom_call" | custom-call | tf_op jit(solution)/shard_map/prep/pallas_call | solution.py:442
  2.5 0.0 copy-start
  2.5 0.5 collective-permute-start.4
  3.0 1.5 %collective-permute-start.3 = (bf16[8,128,128]{2,1,0:T(8,128)(2,1)}, bf16[8,128,128]{2,1,0:T(8,128)(2,1)S(1)}, u32[]{:S(2)}, u32[]{:S(2)}) collective-permute-start(bf16[8,128,128]{2,1,0:T(8,128)(2,1)} %prep.1.refs_0_), channel_id=1, source_target_pairs={{0,16},{8,24},{16,0},{24,8},{1,17},{9,25},{17,1},{25,9},{2,18},{10... | collective-permute-start | bytes 786440 | tf_op jit(solution)/shard_map/ppermute | solution.py:450
  4.6 2.4 %collective-permute-start.2 = (bf16[8,128,128]{2,1,0:T(8,128)(2,1)}, bf16[8,128,128]{2,1,0:T(8,128)(2,1)S(1)}, u32[]{:S(2)}, u32[]{:S(2)}) collective-permute-start(bf16[8,128,128]{2,1,0:T(8,128)(2,1)} %prep.1.refs_0_), channel_id=1, source_target_pairs={{0,8},{8,16},{16,24},{24,0},{1,9},{9,17},{17,25},{25,1},{2,10},{10... | collective-permute-start | bytes 786440 | tf_op jit(solution)/shard_map/ppermute | solution.py:450
  7.6 0.0 copy-start.1
  7.6 0.7 copy-done.1
  8.3 0.0 copy-start.2
  8.3 0.7 copy-done.2
  9.0 1.3 order.1.order_ref.order_a
  10.3 0.1 collective-permute-start
  10.4 0.0 copy-start.3
  10.4 1.2 copy-done.3
  11.6 15.8 %build.2 = (bf16[576,256,128]{2,1,0:T(8,128)(2,1)}, f32[32,128]{1,0:T(8,128)S(1)}) custom-call(s32[8,1152]{1,0:T(8,128)S(1)} %order.1.order_ref.order_a, s32[2,1024,128]{2,1,0:T(8,128)S(1)} %bitcast.10, s32[2,1024,128]{2,1,0:T(8,128)S(1)} %bitcast.11), custom_call_target="tpu_custom_call" | custom-call | flops 10000000000 | tf_op jit(solution)/shard_map/build/pallas_call | solution.py:466
  27.4 0.0 collective-permute-done.order_ref.order_b
  27.4 0.0 collective-permute-done.1
  27.4 7.6 %build.3 = (bf16[576,256,128]{2,1,0:T(8,128)(2,1)}, f32[32,128]{1,0:T(8,128)S(1)}) custom-call(s32[8,1152]{1,0:T(8,128)S(1)} %collective-permute-done.order_ref.order_b, s32[2,1024,128]{2,1,0:T(8,128)S(1)} %bitcast.12, s32[2,1024,128]{2,1,0:T(8,128)S(1)} %bitcast.13), custom_call_target="tpu_custom_call" | custom-call | flops 10000000000 | tf_op jit(solution)/shard_map/build/pallas_call | solution.py:466
  35.1 0.0 collective-permute-done.4.refs_3_
  35.1 0.0 collective-permute-done.3.refs_2_
  35.1 0.0 collective-permute-done.2.refs_1_
  35.1 0.0 copy-done
  35.1 6.3 %start.1 = (bf16[64,128,128]{2,1,0:T(8,128)(2,1)S(1)}, f32[8,128]{1,0:T(8,128)S(1)}) custom-call(f32[32,128]{1,0:T(8,128)S(1)} %get-tuple-element.12.deg_a_ref, f32[32,128]{1,0:T(8,128)S(1)} %get-tuple-element.13.deg_b_ref, bf16[8,128,128]{2,1,0:T(8,128)(2,1)S(1)} %copy-done, bf16[8,128,128]{2,1,0:T(8,128)(2,1)S(1)} %collective-permute-done.2.refs_1_, ...), custom_call_target="tpu_custom_call" | custom-call | tf_op jit(solution)/shard_map/start/pallas_call | solution.py:493
  41.5 14.1 %apply.2.part_ref = bf16[32,128,128]{2,1,0:T(8,128)(2,1)S(1)} custom-call(s32[8,1152]{1,0:T(8,128)S(1)} %order.1.order_ref.order_a, s32[8,1152]{1,0:T(8,128)S(1)} %collective-permute-done.order_ref.order_b, bf16[576,256,128]{2,1,0:T(8,128)(2,1)} %get-tuple-element.10.store_a, bf16[576,256,128]{2,1,0:T(8,128)(2,1)} %get-tuple-element.11.store_b, ...), custom_call_target="tpu_custom_call" | custom-call | tf_op jit(solution)/shard_map/apply/pallas_call | solution.py:518
  55.6 43.6 %spread.1 = (bf16[1024,128]{1,0:T(8,128)(2,1)S(1)}, bf16[64,128,128]{2,1,0:T(8,128)(2,1)S(1)}) custom-call(bf16[32,128,128]{2,1,0:T(8,128)(2,1)S(1)} %apply.2.part_ref, f32[8,128]{1,0:T(8,128)S(1)} %get-tuple-element.15.root_ref), custom_call_target="tpu_custom_call" | custom-call | tf_op jit(solution)/shard_map/spread/pallas_call | solution.py:539
  99.2 14.1 %apply.3.part_ref = bf16[32,128,128]{2,1,0:T(8,128)(2,1)S(1)} custom-call(s32[8,1152]{1,0:T(8,128)S(1)} %order.1.order_ref.order_a, s32[8,1152]{1,0:T(8,128)S(1)} %collective-permute-done.order_ref.order_b, bf16[576,256,128]{2,1,0:T(8,128)(2,1)} %get-tuple-element.10.store_a, bf16[576,256,128]{2,1,0:T(8,128)(2,1)} %get-tuple-element.11.store_b, ...), custom_call_target="tpu_custom_call" | custom-call | tf_op jit(solution)/shard_map/apply/pallas_call | solution.py:518
  113.4 34.0 %finish.1 = bf16[1024,128]{1,0:T(8,128)(2,1)S(1)} custom-call(bf16[32,128,128]{2,1,0:T(8,128)(2,1)S(1)} %apply.3.part_ref, f32[8,128]{1,0:T(8,128)S(1)} %get-tuple-element.15.root_ref), custom_call_target="tpu_custom_call" | custom-call | tf_op jit(solution)/shard_map/finish/pallas_call | solution.py:539
  147.4 0.7 copy.11
  148.1 0.7 copy.12
Async XLA Ops:
  0.6 26.8 %collective-permute-start.1 = (s32[2,1,1,1024,128]{4,3,0,2,1:T(8,128)}, s32[2,1,1,1024,128]{4,3,0,2,1:T(8,128)S(1)}, u32[]{:S(2)}, u32[]{:S(2)}) collective-permute-start(s32[2,1,1,1024,128]{4,3,0,2,1:T(8,128)} %bitcast.9), channel_id=1, source_target_pairs={{0,1},{1,0},{2,3},{3,2},{4,5},{5,4},{6,7},{7,6},{8,9},{9,8},{10,11... | collective-permute-start | bytes 3145736 | tf_op jit(solution)/shard_map/ppermute | solution.py:440
  2.5 32.6 %copy-start = (bf16[8,128,128]{2,1,0:T(8,128)(2,1)S(1)}, bf16[8,128,128]{2,1,0:T(8,128)(2,1)}, u32[]{:S(2)}) copy-start(bf16[8,128,128]{2,1,0:T(8,128)(2,1)} %prep.1.refs_0_) | copy-start | bytes 786436
  2.5 32.6 %collective-permute-start.4 = (bf16[8,128,128]{2,1,0:T(8,128)(2,1)}, bf16[8,128,128]{2,1,0:T(8,128)(2,1)S(1)}, u32[]{:S(2)}, u32[]{:S(2)}) collective-permute-start(bf16[8,128,128]{2,1,0:T(8,128)(2,1)} %prep.1.refs_0_), channel_id=1, source_target_pairs={{0,24},{8,0},{16,8},{24,16},{1,25},{9,1},{17,9},{25,17},{2,26},{10... | collective-permute-start | bytes 786440 | tf_op jit(solution)/shard_map/ppermute | solution.py:450
  3.0 32.0 %collective-permute-start.3 = (bf16[8,128,128]{2,1,0:T(8,128)(2,1)}, bf16[8,128,128]{2,1,0:T(8,128)(2,1)S(1)}, u32[]{:S(2)}, u32[]{:S(2)}) collective-permute-start(bf16[8,128,128]{2,1,0:T(8,128)(2,1)} %prep.1.refs_0_), channel_id=1, source_target_pairs={{0,16},{8,24},{16,0},{24,8},{1,17},{9,25},{17,1},{25,9},{2,18},{10... | collective-permute-start | bytes 786440 | tf_op jit(solution)/shard_map/ppermute | solution.py:450
  4.6 30.5 %collective-permute-start.2 = (bf16[8,128,128]{2,1,0:T(8,128)(2,1)}, bf16[8,128,128]{2,1,0:T(8,128)(2,1)S(1)}, u32[]{:S(2)}, u32[]{:S(2)}) collective-permute-start(bf16[8,128,128]{2,1,0:T(8,128)(2,1)} %prep.1.refs_0_), channel_id=1, source_target_pairs={{0,8},{8,16},{16,24},{24,0},{1,9},{9,17},{17,25},{25,1},{2,10},{10... | collective-permute-start | bytes 786440 | tf_op jit(solution)/shard_map/ppermute | solution.py:450
  7.6 0.7 copy-start.1
  8.3 0.7 copy-start.2
  10.3 17.1 %collective-permute-start = (s32[8,1152]{1,0:T(8,128)S(1)}, s32[8,1152]{1,0:T(8,128)S(1)}, u32[]{:S(2)}, u32[]{:S(2)}) collective-permute-start(s32[8,1152]{1,0:T(8,128)S(1)} %order.1.order_ref.order_a), channel_id=1, source_target_pairs={{0,1},{1,0},{2,3},{3,2},{4,5},{5,4},{6,7},{7,6},{8,9},{9,8},{10,11... | collective-permute-start | bytes 110600 | tf_op jit(solution)/shard_map/ppermute | solution.py:462
  10.4 1.2 copy-start.3
where the time goes:
time: 151 us; the launch traced here: 149 us
  Pallas kernels  139 us (92%)
  starting transfers between devices  4.59 us (3%)
  local copies, waits for them, and re-layouts  4 us (3%)
    pallas_call x2, Pallas kernels, collect(): pl.pallas_call(functools.partial(sum_kernel, n_row, n_col, spread), out_s...  77.6 us
    pallas_call x2, Pallas kernels, apply(): pl.pallas_call(body, in_specs=[SMEM_SPEC] * 2 + [ANY_SPEC] * 2 + [VMEM_SP...  28.3 us
    pallas_call x2, Pallas kernels, build(): pl.pallas_call(functools.partial(build_kernel, half_tiles, other), in_spe...  23.4 us
    pallas_call x1, Pallas kernels, local(): pl.pallas_call(functools.partial(start_kernel, n_row, n_col), out_shape=[...  6.33 us
    ppermute x3, starting transfers between devices, local(): lax.ppermute(turned, 'row', [(i, (i + d) % n_row) for i in range(n_row)])  4.44 us
    unnamed x10, local copies, waits for them, and re-layouts  4 us
  transfers between devices with their start and end apart: 5, of which 0 were waited for; matrix products, arithmetic and copies ran while one was open for 0% of the time, Pallas kernels for 18%

commit v1 on v0

--- a/solution.py
+++ b/solution.py
@@ -13,9 +13,10 @@
 APPLY_UNROLL = 32
 APPLY_SLOTS = 4
 HOT = jnp.float8_e4m3fn
-HOT_EXTRA = 32
+HOT_ROWS = 32
 EXTRA = 16
 PIECES = 4
+RELAY_LAG = 3
 CORES = 2
 MESH_ID = pl.DeviceIdType.MESH
 VMEM_SPEC = pl.BlockSpec(memory_space=pltpu.VMEM)
@@ -94,7 +95,16 @@
     low, high = span_of(order_ref, half_bins, other)
     turns = (high - low + BUILD_UNROLL - 1) // BUILD_UNROLL
     pairs = BUILD_UNROLL // 2
-    cells = lax.broadcasted_iota(jnp.int32, (TILE, TILE), 0)
+    cells = [
+        (lax.broadcasted_iota(jnp.int32, (HOT_ROWS, TILE), 0) + start).astype(jnp.int8)
+        for start in range(0, TILE, HOT_ROWS)
+    ]
+
+    def hot(ids):
+        ids = jnp.broadcast_to(ids, (HOT_ROWS, TILE)).astype(jnp.int8)
+        return jnp.concatenate(
+            [jnp.where(ids == cell, HOT(1), HOT(0)) for cell in cells], axis=0
+        )
 
     def out_copy(turn):
         side = lax.rem(turn, 2)
@@ -117,15 +127,11 @@
                 safe = jnp.maximum(slot, 0)
                 dst = jnp.where(slot >= 0, dst_ref[pl.ds(safe, 1), :], -1)
                 src = src_ref[pl.ds(safe, 1), :]
-                dst_hot = jnp.where(dst == cells, 1.0, 0.0).astype(HOT)
-                src_hot = jnp.where(src == cells, 1.0, 0.0).astype(HOT)
-                valid = jnp.broadcast_to(jnp.where(src >= 0, 1.0, 0.0), (HOT_EXTRA, TILE))
-                left = jnp.concatenate([src_hot, valid.astype(HOT)], axis=0)
                 both = lax.dot_general(
-                    left, dst_hot, (((1,), (1,)), ((), ())), preferred_element_type=jnp.float32
+                    hot(src), hot(dst), (((1,), (1,)), ((), ())), preferred_element_type=jnp.float32
                 )
-                made[side, pair, half * TILE : (half + 1) * TILE] = both[:TILE].astype(jnp.bfloat16)
-                counts.append(both[TILE : TILE + 8])
+                made[side, pair, half * TILE : (half + 1) * TILE] = both.astype(jnp.bfloat16)
+                counts.append(jnp.sum(both.reshape(TILE // 8, 8, TILE), axis=0))
             degree_acc[order_ref[1, base]] += counts[0] + counts[1]
         out_copy(turn).start()
         return carry
@@ -140,7 +146,7 @@
     def _():
         out_copy(turns - 1).wait()
 
-    degree_ref[...] = degree_acc[:, 0, :]
+    degree_ref[...] = jnp.sum(degree_acc[...], axis=1)
 
 
 def apply_kernel(half_bins, orders, stores, source_ref, out_ref, held, acc, sem):
@@ -318,27 +324,32 @@
     greet([up, down] + ([partner] + mine if spread else []))
     last = n_chip - 1
 
+    low_half = chip < n_chip // 2
+    early = jnp.where(low_half, 0, 1)
+
     def hop_copy(way, k, piece, direct):
-        target = last - k if way == 0 else k
-        source = (
-            part_ref.at[pl.ds(target * own + piece * size, size)] if direct else goes.at[way, k, piece]
-        )
+        target = jnp.where(way == 0, last - k, k)
+        start = pl.multiple_of(target * own, own) + piece * size
+        source = part_ref.at[pl.ds(start, size)] if direct else goes.at[way, k, piece]
         return remote(
             source,
             comes.at[way, k, piece],
             send_sem.at[way, k, piece],
             recv_sem.at[way, k, piece],
-            down if way else up,
+            (row, lax.rem(col + jnp.where(way == 0, CORES, n_col - CORES), n_col)),
         )
 
+    flow = [(k, piece) for k in range(last) for piece in range(PIECES)]
+    timed = [(i, 0, *f) for i, f in enumerate(flow)]
+    timed += [(i + RELAY_LAG, 1, *f) for i, f in enumerate(flow)]
+
     def steps():
-        for k in range(last):
-            for piece in range(PIECES):
-                for way in range(2):
-                    target = last - k if way == 0 else k
-                    ahead = (chip < target) if way == 0 else (chip > target)
-                    first = chip == (0 if way == 0 else last)
-                    yield k, piece, way, target, ahead, first
+        for _, late, k, piece in sorted(timed):
+            way = 1 - early if late else early
+            target = jnp.where(way == 0, last - k, k)
+            ahead = jnp.where(way == 0, target - chip, chip - target) > 0
+            first = chip == jnp.where(way == 0, 0, last)
+            yield k, piece, way, target, ahead, first
 
     for k, piece, way, target, ahead, first in steps():
 
@@ -349,9 +360,9 @@
         @pl.when(ahead & jnp.logical_not(first))
         def _():
             hop_copy(way, k, piece, False).wait_recv()
-            start = target * own + piece * size
+            start = pl.multiple_of(target * own, own) + piece * size
             goes[way, k, piece] = (
-                part_ref[start : start + size].astype(jnp.float32)
+                part_ref[pl.ds(start, size)].astype(jnp.float32)
                 + comes[way, k, piece].astype(jnp.float32)
             ).astype(jnp.bfloat16)
             hop_copy(way, k, piece, False).start()

time: 151 us -> 116 us (0.77)
  the two profiles are of different devices: /device:TPU:18 before, /device:TPU:14 now
where the time goes in v1:
time: 116 us; the launch traced here: 115 us
  Pallas kernels  106 us (91%)
  local copies, waits for them, and re-layouts  4 us (3%)
  starting transfers between devices  3.58 us (3%)
  between operations  1.42 us (1%)
    pallas_call x2, Pallas kernels, collect(): pl.pallas_call(functools.partial(sum_kernel, n_row, n_col, spread), out_s...  51.5 us
    pallas_call x2, Pallas kernels, apply(): pl.pallas_call(body, in_specs=[SMEM_SPEC] * 2 + [ANY_SPEC] * 2 + [VMEM_SP...  26.4 us
    pallas_call x2, Pallas kernels, build(): pl.pallas_call(functools.partial(build_kernel, half_tiles, other), in_spe...  19 us
    pallas_call x1, Pallas kernels, local(): pl.pallas_call(functools.partial(start_kernel, n_row, n_col), out_shape=[...  6.33 us
    unnamed x10, local copies, waits for them, and re-layouts  4 us
    ppermute x3, starting transfers between devices, local(): lax.ppermute(turned, 'row', [(i, (i + d) % n_row) for i in range(n_row)])  3.43 us
  transfers between devices with their start and end apart: 5, of which 0 were waited for; matrix products, arithmetic and copies ran while one was open for 0% of the time, Pallas kernels for 19%

profile of v1, /device:TPU:14, one launch (start us, length us, event | category | flops | bytes accessed | tf_op | source)
XLA Modules:
  0.0 115.4 jit_solution(15735251440289627199)
XLA Ops:
  0.6 0.1 collective-permute-start.1
  0.7 1.8 %prep.1.refs_0_ = bf16[8,128,128]{2,1,0:T(8,128)(2,1)} custom-call(bf16[1024,128]{1,0:T(8,128)(2,1)} %features_ref.1), custom_call_target="tpu_custom_call" | custom-call | tf_op jit(solution)/shard_map/prep/pallas_call | solution.py:453
  2.5 0.0 copy-start
  2.5 0.5 collective-permute-start.4
  3.0 0.5 collective-permute-start.3
  3.5 2.4 %collective-permute-start.2 = (bf16[8,128,128]{2,1,0:T(8,128)(2,1)}, bf16[8,128,128]{2,1,0:T(8,128)(2,1)S(1)}, u32[]{:S(2)}, u32[]{:S(2)}) collective-permute-start(bf16[8,128,128]{2,1,0:T(8,128)(2,1)} %prep.1.refs_0_), channel_id=1, source_target_pairs={{0,8},{8,16},{16,24},{24,0},{1,9},{9,17},{17,25},{25,1},{2,10},{10... | collective-permute-start | bytes 786440 | tf_op jit(solution)/shard_map/ppermute | solution.py:461
  6.6 0.0 copy-start.1
  6.6 0.7 copy-done.1
  7.3 0.0 copy-start.2
  7.3 0.7 copy-done.2
  8.0 1.3 %order.1.order_ref.order_a = s32[8,1152]{1,0:T(8,128)S(1)} custom-call(s32[1]{0:T(128)} %bitcast.6.count_ref, s32[1,1024]{1,0:T(1,128)S(1)} %bitcast.7, s32[1,1024]{1,0:T(1,128)S(1)} %bitcast.8), custom_call_target="tpu_custom_call" | custom-call | tf_op jit(solution)/shard_map/order/pallas_call | solution.py:465
  9.3 0.1 collective-permute-start
  9.4 0.0 copy-start.3
  9.4 1.2 %copy-done.3 = s32[2,1,1,1024,128]{4,3,2,1,0:T(8,128)S(1)} copy-done((s32[2,1,1,1024,128]{4,3,2,1,0:T(8,128)S(1)}, s32[2,1,1,1024,128]{4,3,2,1,0:T(8,128)}, u32[]{:S(2)}) %copy-start.3) | copy-done | bytes 1048600
  10.6 5.3 %build.2 = (bf16[576,256,128]{2,1,0:T(8,128)(2,1)}, f32[32,128]{1,0:T(8,128)S(1)}) custom-call(s32[8,1152]{1,0:T(8,128)S(1)} %order.1.order_ref.order_a, s32[2,1024,128]{2,1,0:T(8,128)S(1)} %bitcast.10, s32[2,1024,128]{2,1,0:T(8,128)S(1)} %bitcast.11), custom_call_target="tpu_custom_call" | custom-call | flops 10000000000 | tf_op jit(solution)/shard_map/build/pallas_call | solution.py:477
  15.9 0.0 collective-permute-done.order_ref.order_b
  16.0 0.0 collective-permute-done.1
  16.0 13.7 %build.3 = (bf16[576,256,128]{2,1,0:T(8,128)(2,1)}, f32[32,128]{1,0:T(8,128)S(1)}) custom-call(s32[8,1152]{1,0:T(8,128)S(1)} %collective-permute-done.order_ref.order_b, s32[2,1024,128]{2,1,0:T(8,128)S(1)} %bitcast.12, s32[2,1024,128]{2,1,0:T(8,128)S(1)} %bitcast.13), custom_call_target="tpu_custom_call" | custom-call | flops 10000000000 | tf_op jit(solution)/shard_map/build/pallas_call | solution.py:477
  29.6 0.0 collective-permute-done.4.refs_3_
  29.6 0.0 collective-permute-done.3.refs_2_
  29.7 0.0 collective-permute-done.2.refs_1_
  29.7 0.0 copy-done
  29.7 6.3 %start.1 = (bf16[64,128,128]{2,1,0:T(8,128)(2,1)S(1)}, f32[8,128]{1,0:T(8,128)S(1)}) custom-call(f32[32,128]{1,0:T(8,128)S(1)} %get-tuple-element.12.deg_a_ref, f32[32,128]{1,0:T(8,128)S(1)} %get-tuple-element.13.deg_b_ref, bf16[8,128,128]{2,1,0:T(8,128)(2,1)S(1)} %copy-done, bf16[8,128,128]{2,1,0:T(8,128)(2,1)S(1)} %collective-permute-done.2.refs_1_, ...), custom_call_target="tpu_custom_call" | custom-call | tf_op jit(solution)/shard_map/start/pallas_call | solution.py:504
  36.0 13.2 %apply.2.part_ref = bf16[32,128,128]{2,1,0:T(8,128)(2,1)S(1)} custom-call(s32[8,1152]{1,0:T(8,128)S(1)} %order.1.order_ref.order_a, s32[8,1152]{1,0:T(8,128)S(1)} %collective-permute-done.order_ref.order_b, bf16[576,256,128]{2,1,0:T(8,128)(2,1)} %get-tuple-element.10.store_a, bf16[576,256,128]{2,1,0:T(8,128)(2,1)} %get-tuple-element.11.store_b, ...), custom_call_target="tpu_custom_call" | custom-call | tf_op jit(solution)/shard_map/apply/pallas_call | solution.py:529
  49.2 31.1 %spread.1 = (bf16[1024,128]{1,0:T(8,128)(2,1)S(1)}, bf16[64,128,128]{2,1,0:T(8,128)(2,1)S(1)}) custom-call(bf16[32,128,128]{2,1,0:T(8,128)(2,1)S(1)} %apply.2.part_ref, f32[8,128]{1,0:T(8,128)S(1)} %get-tuple-element.15.root_ref), custom_call_target="tpu_custom_call" | custom-call | tf_op jit(solution)/shard_map/spread/pallas_call | solution.py:550
  80.3 13.2 %apply.3.part_ref = bf16[32,128,128]{2,1,0:T(8,128)(2,1)S(1)} custom-call(s32[8,1152]{1,0:T(8,128)S(1)} %order.1.order_ref.order_a, s32[8,1152]{1,0:T(8,128)S(1)} %collective-permute-done.order_ref.order_b, bf16[576,256,128]{2,1,0:T(8,128)(2,1)} %get-tuple-element.10.store_a, bf16[576,256,128]{2,1,0:T(8,128)(2,1)} %get-tuple-element.11.store_b, ...), custom_call_target="tpu_custom_call" | custom-call | tf_op jit(solution)/shard_map/apply/pallas_call | solution.py:529
  93.6 20.5 %finish.1 = bf16[1024,128]{1,0:T(8,128)(2,1)S(1)} custom-call(bf16[32,128,128]{2,1,0:T(8,128)(2,1)S(1)} %apply.3.part_ref, f32[8,128]{1,0:T(8,128)S(1)} %get-tuple-element.15.root_ref), custom_call_target="tpu_custom_call" | custom-call | tf_op jit(solution)/shard_map/finish/pallas_call | solution.py:550
  114.0 0.7 copy.11
  114.7 0.7 copy.12
Async XLA Ops:
  0.6 15.3 %collective-permute-start.1 = (s32[2,1,1,1024,128]{4,3,0,2,1:T(8,128)}, s32[2,1,1,1024,128]{4,3,0,2,1:T(8,128)S(1)}, u32[]{:S(2)}, u32[]{:S(2)}) collective-permute-start(s32[2,1,1,1024,128]{4,3,0,2,1:T(8,128)} %bitcast.9), channel_id=1, source_target_pairs={{0,1},{1,0},{2,3},{3,2},{4,5},{5,4},{6,7},{7,6},{8,9},{9,8},{10,11... | collective-permute-start | bytes 3145736 | tf_op jit(solution)/shard_map/ppermute | solution.py:451
  2.5 27.2 %copy-start = (bf16[8,128,128]{2,1,0:T(8,128)(2,1)S(1)}, bf16[8,128,128]{2,1,0:T(8,128)(2,1)}, u32[]{:S(2)}) copy-start(bf16[8,128,128]{2,1,0:T(8,128)(2,1)} %prep.1.refs_0_) | copy-start | bytes 786436
  2.5 27.1 %collective-permute-start.4 = (bf16[8,128,128]{2,1,0:T(8,128)(2,1)}, bf16[8,128,128]{2,1,0:T(8,128)(2,1)S(1)}, u32[]{:S(2)}, u32[]{:S(2)}) collective-permute-start(bf16[8,128,128]{2,1,0:T(8,128)(2,1)} %prep.1.refs_0_), channel_id=1, source_target_pairs={{0,24},{8,0},{16,8},{24,16},{1,25},{9,1},{17,9},{25,17},{2,26},{10... | collective-permute-start | bytes 786440 | tf_op jit(solution)/shard_map/ppermute | solution.py:461
  3.0 26.6 %collective-permute-start.3 = (bf16[8,128,128]{2,1,0:T(8,128)(2,1)}, bf16[8,128,128]{2,1,0:T(8,128)(2,1)S(1)}, u32[]{:S(2)}, u32[]{:S(2)}) collective-permute-start(bf16[8,128,128]{2,1,0:T(8,128)(2,1)} %prep.1.refs_0_), channel_id=1, source_target_pairs={{0,16},{8,24},{16,0},{24,8},{1,17},{9,25},{17,1},{25,9},{2,18},{10... | collective-permute-start | bytes 786440 | tf_op jit(solution)/shard_map/ppermute | solution.py:461
  3.5 26.1 %collective-permute-start.2 = (bf16[8,128,128]{2,1,0:T(8,128)(2,1)}, bf16[8,128,128]{2,1,0:T(8,128)(2,1)S(1)}, u32[]{:S(2)}, u32[]{:S(2)}) collective-permute-start(bf16[8,128,128]{2,1,0:T(8,128)(2,1)} %prep.1.refs_0_), channel_id=1, source_target_pairs={{0,8},{8,16},{16,24},{24,0},{1,9},{9,17},{17,25},{25,1},{2,10},{10... | collective-permute-start | bytes 786440 | tf_op jit(solution)/shard_map/ppermute | solution.py:461
  6.6 0.7 copy-start.1
  7.3 0.7 copy-start.2
  9.3 6.6 %collective-permute-start = (s32[8,1152]{1,0:T(8,128)S(1)}, s32[8,1152]{1,0:T(8,128)S(1)}, u32[]{:S(2)}, u32[]{:S(2)}) collective-permute-start(s32[8,1152]{1,0:T(8,128)S(1)} %order.1.order_ref.order_a), channel_id=1, source_target_pairs={{0,1},{1,0},{2,3},{3,2},{4,5},{5,4},{6,7},{7,6},{8,9},{9,8},{10,11... | collective-permute-start | bytes 110600 | tf_op jit(solution)/shard_map/ppermute | solution.py:473
  9.4 1.2 %copy-start.3 = (s32[2,1,1,1024,128]{4,3,2,1,0:T(8,128)S(1)}, s32[2,1,1,1024,128]{4,3,2,1,0:T(8,128)}, u32[]{:S(2)}) copy-start(s32[2,1,1,1024,128]{4,3,2,1,0:T(8,128)} %param.8) | copy-start | bytes 3145732
